TPU v7x, 32 devices: a whole 2x2x4 slice. The times are simulated.
32 devices in a mesh: section: 4 (over y, x), dp: 8 (over z, core).
Axes of the slice: x: 2, y: 2, z: 4, core: 2. Of those that a mesh axis runs over, the one named last changes fastest.
Arguments:
- clip_pool: bfloat16 [256, 256, 512], P('dp'), may hold values from -8 to 8
- clip_index: int32 [8, 32], P(None, 'dp'), may hold values from 0 to 31, as said below
- batch_order: int32 [8], replicated, may hold values from 0 to 7, each once
- tap_weights: bfloat16 [4, 3, 512, 512], P('section'), may hold values from -0.15625 to 0.15625
- out_weights: bfloat16 [4, 512, 512], P('section'), may hold values from -0.25 to 0.25
- norm_gains: bfloat16 [4, 512], P('section'), may hold values from 0.099609375 to 1.8984375
- quant_weight: bfloat16 [512, 18], replicated, may hold values from -0.25 to 0.25
- quant_bias: float32 [18], replicated, may hold values from -3 to 3
- post_weight: bfloat16 [18, 512], replicated, may hold values from -1.5 to 1.5
Outputs:
- row_error: float32 [8, 32, 256], P('section', 'dp')
- entropy_loss: float32 [8], replicated
Inputs may be any that keep to these rules, and one draw needn't show every extreme that they name: `clip_index`: entries index the clips of the replica that holds the column; over all 8 micro-batches, the 4 columns of one replica name each of its 32 clips exactly once. `batch_order`: each micro-batch number 0 to 7 once.
All inputs are finite; a program needn't handle non-finite values.
Results may differ from a plain program's by a relative error of at most 0.0015.
Values may be sent and summed in bfloat16 or wider, within the bound.
A program may use at most 128 MiB of HBM per device.

v0:
```python
import jax
import jax.numpy as jnp
from jax import lax
from jax.sharding import PartitionSpec as P

SPATIAL = 64
norm_eps = 1e-06
quant_section = 1


def run_block(current, tap_set, out_weight, gain_row):
    clip_count, row_count, channels = current.shape
    widened = current.astype(jnp.float32)
    scale = lax.rsqrt(jnp.mean(widened * widened, axis=-1, keepdims=True) + norm_eps)
    normed = (widened * scale * gain_row.astype(jnp.float32)).astype(jnp.bfloat16)
    flat = normed.reshape(-1, channels)
    mixed = jnp.zeros((clip_count, row_count, channels), jnp.float32)
    for k in range(tap_set.shape[0]):
        product = jnp.dot(flat, tap_set[k], preferred_element_type=jnp.float32).reshape(
            clip_count, row_count, channels
        )
        moved = jnp.pad(product, ((0, 0), (k * SPATIAL, 0), (0, 0)))[:, :row_count]
        mixed = mixed + moved
    activated = jax.nn.silu(mixed).astype(jnp.bfloat16)
    update = jnp.dot(
        activated.reshape(-1, channels), out_weight, preferred_element_type=jnp.float32
    )
    return (widened + update.reshape(clip_count, row_count, channels)).astype(jnp.bfloat16)


def quantize(current, quant_weight, quant_bias, post_weight):
    channels = current.shape[-1]
    logits = (
        jnp.dot(current.reshape(-1, channels), quant_weight, preferred_element_type=jnp.float32)
        + quant_bias
    )
    bit_prob = jax.nn.sigmoid(4.0 * logits)
    codes = (2.0 * bit_prob - 1.0).astype(jnp.bfloat16)
    quantized = jnp.dot(codes, post_weight, preferred_element_type=jnp.float32).astype(jnp.bfloat16)
    bit_sums = jnp.sum(bit_prob, axis=0)
    entropy_sum = -jnp.sum(
        bit_prob * jax.nn.log_sigmoid(4.0 * logits)
        + (1.0 - bit_prob) * jax.nn.log_sigmoid(-4.0 * logits)
    )
    return (quantized.reshape(current.shape), bit_sums, entropy_sum)


def squared_error(decoded, source):
    differ = decoded.astype(jnp.float32) - source.astype(jnp.float32)
    return jnp.mean(differ * differ, axis=-1)


def final_entropy(bit_buffer, entropy_buffer, batch_order, rows_total):
    marginal = bit_buffer / rows_total
    sample_entropy = entropy_buffer / rows_total
    averaged = jnp.zeros_like(marginal)
    running = marginal[batch_order[0]]
    for t in range(batch_order.shape[0]):
        if t > 0:
            running = 0.5 * running + 0.5 * marginal[batch_order[t]]
        averaged = averaged.at[batch_order[t]].set(running)
    smoothed = 0.05 + 0.9 * averaged
    code_entropy = -jnp.sum(
        smoothed * jnp.log(smoothed) + (1.0 - smoothed) * jnp.log(1.0 - smoothed), axis=-1
    )
    return sample_entropy - code_entropy


def on_device(
    clip_pool,
    clip_index,
    batch_order,
    tap_weights,
    out_weights,
    norm_gains,
    quant_weight,
    quant_bias,
    post_weight,
):
    section_id = lax.axis_index("section")
    sections = lax.axis_size("section")
    batches = batch_order.shape[0]
    clip_count = clip_index.shape[1]
    row_count = clip_pool.shape[1]
    rows_total = float(clip_count * lax.axis_size("dp") * row_count)
    bit_buffer = jnp.zeros((batches, quant_weight.shape[1]), jnp.float32)
    entropy_buffer = jnp.zeros((batches,), jnp.float32)
    all_taps, all_out, all_gains = (
        lax.all_gather(tap_weights, "section", axis=0, tiled=True),
        lax.all_gather(out_weights, "section", axis=0, tiled=True),
        lax.all_gather(norm_gains, "section", axis=0, tiled=True),
    )
    per_section = batches // sections
    error_list = []
    for i in range(per_section):
        batch_slot = section_id * per_section + i
        source = jnp.take(clip_pool, clip_index[batch_slot], axis=0)
        current = source
        for s in range(sections):
            current = run_block(current, all_taps[s], all_out[s], all_gains[s])
            if s == quant_section:
                current, bit_sums, entropy_sum = quantize(
                    current, quant_weight, quant_bias, post_weight
                )
                bit_buffer = bit_buffer.at[batch_slot].add(bit_sums)
                entropy_buffer = entropy_buffer.at[batch_slot].add(entropy_sum)
        error_list.append(squared_error(current, source))
    bit_buffer, entropy_buffer = lax.psum((bit_buffer, entropy_buffer), ("section", "dp"))
    error_out = jnp.stack(error_list)
    losses = final_entropy(bit_buffer, entropy_buffer, batch_order, rows_total)
    return (error_out, losses)


def solution(mesh):
    placed = (
        P("dp", None, None),
        P(None, "dp"),
        P(),
        P("section", None, None, None),
        P("section", None, None),
        P("section", None),
        P(),
        P(),
        P(),
    )
    return jax.shard_map(
        on_device,
        mesh=mesh,
        in_specs=placed,
        out_specs=(P("section", "dp", None), P()),
        check_vma=False,
    )
```

profile of v0, /device:TPU:0, one launch (start us, length us, event | category | flops | bytes accessed | tf_op | source)
XLA Modules:
  0.0 263.3 jit_solution(17527668626507960612)
XLA Ops:
  7.2 0.0 copy-start
  7.2 0.0 all-gather.4.cloned.1.call-start
  7.2 0.7 all-gather.4.cloned.1.call-update
  7.9 0.0 all-gather.6.cloned.1.call-start
  8.0 0.7 all-gather.6.cloned.1.call-update
  8.7 0.7 fusion.181
  19.8 0.2 fusion.140
  20.1 0.0 copy-start.9
  20.1 4.9 %gather_fusion = bf16[4,256,512]{2,1,0:T(8,128)(2,1)S(1)} fusion(bf16[32,256,512]{2,1,0:T(8,128)(2,1)} %param.35, s32[1024]{0:T(1024)S(1)} %pad_clamp_fusion.1), kind=kCustom, calls=%fused_computation.clone | custom fusion | bytes 2097168 | tf_op jit(solution)/shard_map/jit(_take)/gather | solution.py:97
  25.0 4.4 %gather_fusion.1 = bf16[4,256,512]{2,1,0:T(8,128)(2,1)S(1)} fusion(bf16[32,256,512]{2,1,0:T(8,128)(2,1)} %param.35, s32[1024]{0:T(1024)S(1)} %pad_clamp_fusion), kind=kCustom, calls=%fused_computation.1.clone | custom fusion | bytes 2097168 | tf_op jit(solution)/shard_map/jit(_take)/gather | solution.py:97
  34.6 9.3 %all-gather = bf16[4,1,512]{2,1,0:T(2,128)(2,1)S(1)} all-gather(bf16[1,1,512]{2,1,0:T(2,128)(2,1)S(1)} %bitcast.176), channel_id=1, replica_groups=mesh['section'=4,'dp'=8] {'section'}, dimensions={0}, use_global_device_ids=true | all-gather | bytes 5120 | tf_op jit(solution)/shard_map/all_gather | solution.py:91
  44.0 0.8 and_reduce_fusion.4
  44.8 0.9 and_reduce_fusion
  45.7 0.4 fusion.32
  46.1 0.4 fusion.38
  46.5 36.1 %all-gather.4.cloned.1.call-done = bf16[4,3,512,512]{3,2,1,0:T(8,128)(2,1)} async-done(((bf16[1,3,512,512]{3,2,1,0:T(8,128)(2,1)}), bf16[4,3,512,512]{3,2,1,0:T(8,128)(2,1)}) %all-gather.4.cloned.1.call-update) | async-done | bytes 6291472 | tf_op jit(solution)/shard_map/all_gather | solution.py:89
  82.7 3.1 %fusion.60 = f32[4,256,512]{2,1,0:T(8,128)} fusion(f32[4,256]{1,0:T(4,128)S(1)} %add_rsqrt_fusion.3, f32[512]{0:T(512)S(1)} %bitcast.189, bf16[4,3,512,512]{3,2,1,0:T(8,128)(2,1)} %all-gather.4.cloned.1.call-done, bf16[4,256,512]{2,1,0:T(8,128)(2,1)S(1)} %gather_fusion.1, pred[4]{0:T(512)(128)(4,1)S(1)} %get-tuple-element.203), kind=kOutput, calls=%fused_computation.107 | convolution fusion | flops 539492352 | bytes 3676164 | tf_op jit(solution)/shard_map/dot_general | solution.py:19
  85.8 3.2 %fusion.58 = f32[4,256,512]{2,1,0:T(8,128)} fusion(f32[4,256]{1,0:T(4,128)S(1)} %add_rsqrt_fusion.3, f32[512]{0:T(512)S(1)} %bitcast.190, bf16[4,3,512,512]{3,2,1,0:T(8,128)(2,1)} %all-gather.4.cloned.1.call-done, bf16[4,256,512]{2,1,0:T(8,128)(2,1)S(1)} %gather_fusion.1, pred[4]{0:T(512)(128)(4,1)S(1)} %get-tuple-element.203), kind=kOutput, calls=%fused_computation.106 | convolution fusion | flops 539492352 | bytes 3676164 | tf_op jit(solution)/shard_map/dot_general | solution.py:19
  89.0 30.7 %all-gather.6.cloned.1.call-done = bf16[4,512,512]{2,1,0:T(8,128)(2,1)} async-done(((bf16[1,512,512]{2,1,0:T(8,128)(2,1)}), bf16[4,512,512]{2,1,0:T(8,128)(2,1)}) %all-gather.6.cloned.1.call-update) | async-done | bytes 2097168 | tf_op jit(solution)/shard_map/all_gather | solution.py:90
  119.7 4.6 %fusion.24 = (f32[4,256]{1,0:T(4,128)S(1)}, bf16[4,256,512]{2,1,0:T(8,128)(2,1)}) fusion(bf16[4,512,512]{2,1,0:T(8,128)(2,1)} %all-gather.6.cloned.1.call-done, f32[4,256,512]{2,1,0:T(8,128)} %fusion.58, f32[4,256,512]{2,1,0:T(8,128)} %fusion.60, f32[4,256]{1,0:T(4,128)S(1)} %add_rsqrt_fusion.3, f32[512]{0:T(512)S(1)} %bitcast.191, ...), kind=kOutput, calls=%fused_computation.62 | convolution fusion | flops 1083702272 | bytes 8399872 | tf_op jit(solution)/shard_map/dot_general | solution.py:25
  124.3 3.5 %fusion.54 = f32[4,256,512]{2,1,0:T(8,128)} fusion(bf16[4,256,512]{2,1,0:T(8,128)(2,1)} %get-tuple-element.188, f32[4,256]{1,0:T(4,128)S(1)} %add_rsqrt_fusion.2, f32[512]{0:T(512)S(1)} %bitcast.183, bf16[4,3,512,512]{3,2,1,0:T(8,128)(2,1)} %all-gather.4.cloned.1.call-done), kind=kOutput, calls=%fused_computation.105 | convolution fusion | flops 538968064 | bytes 3676160 | tf_op jit(solution)/shard_map/dot_general | solution.py:19
  127.9 3.2 %fusion.52 = f32[4,256,512]{2,1,0:T(8,128)} fusion(bf16[4,256,512]{2,1,0:T(8,128)(2,1)S(1)} %copy-done.16, f32[4,256]{1,0:T(4,128)S(1)} %add_rsqrt_fusion.2, f32[512]{0:T(512)S(1)} %bitcast.184, bf16[4,3,512,512]{3,2,1,0:T(8,128)(2,1)} %all-gather.4.cloned.1.call-done), kind=kOutput, calls=%fused_computation.104 | convolution fusion | flops 538968064 | bytes 3676160 | tf_op jit(solution)/shard_map/dot_general | solution.py:19
  131.1 5.2 %fusion.27 = bf16[4,256,512]{2,1,0:T(8,128)(2,1)} fusion(bf16[4,256,512]{2,1,0:T(8,128)(2,1)} %get-tuple-element.188, f32[4,256,512]{2,1,0:T(8,128)} %fusion.52, f32[4,256,512]{2,1,0:T(8,128)} %fusion.54, f32[4,256]{1,0:T(4,128)S(1)} %add_rsqrt_fusion.2, f32[512]{0:T(512)S(1)} %bitcast.185, bf16[4,3,512,512]{3,2,1,0:T(8,128)(2,1)} %all-gather.4.cloned.1.call-done, ...), kind=kOutput, calls=%fused_computation.65 | convolution fusion | flops 1081081856 | bytes 8394752 | tf_op jit(solution)/shard_map/dot_general | solution.py:25
  136.2 2.4 fusion.131
  139.3 3.2 %fusion.104 = f32[4,256,512]{2,1,0:T(8,128)} fusion(f32[512]{0:T(512)S(1)} %bitcast.192, f32[4,256]{1,0:T(4,128)S(1)} %add_rsqrt_fusion.7, bf16[4,3,512,512]{3,2,1,0:T(8,128)(2,1)} %all-gather.4.cloned.1.call-done, bf16[4,256,512]{2,1,0:T(8,128)(2,1)S(1)} %gather_fusion, pred[4]{0:T(512)(128)(4,1)S(1)} %get-tuple-element.204), kind=kOutput, calls=%fused_computation.135 | convolution fusion | flops 539492352 | bytes 3676164 | tf_op jit(solution)/shard_map/dot_general | solution.py:19
  142.5 3.1 %fusion.106 = f32[4,256,512]{2,1,0:T(8,128)} fusion(f32[512]{0:T(512)S(1)} %bitcast.193, f32[4,256]{1,0:T(4,128)S(1)} %add_rsqrt_fusion.7, bf16[4,3,512,512]{3,2,1,0:T(8,128)(2,1)} %all-gather.4.cloned.1.call-done, bf16[4,256,512]{2,1,0:T(8,128)(2,1)S(1)} %gather_fusion, pred[4]{0:T(512)(128)(4,1)S(1)} %get-tuple-element.204), kind=kOutput, calls=%fused_computation.136 | convolution fusion | flops 539492352 | bytes 3676164 | tf_op jit(solution)/shard_map/dot_general | solution.py:19
  145.6 4.6 %fusion.16 = (f32[4,256]{1,0:T(4,128)S(1)}, bf16[4,256,512]{2,1,0:T(8,128)(2,1)}) fusion(bf16[4,512,512]{2,1,0:T(8,128)(2,1)} %all-gather.6.cloned.1.call-done, f32[4,256,512]{2,1,0:T(8,128)} %fusion.104, f32[4,256,512]{2,1,0:T(8,128)} %fusion.106, f32[512]{0:T(512)S(1)} %bitcast.194, f32[4,256]{1,0:T(4,128)S(1)} %add_rsqrt_fusion.7, ...), kind=kOutput, calls=%fused_computation.54 | convolution fusion | flops 1083702272 | bytes 8399872 | tf_op jit(solution)/shard_map/dot_general | solution.py:25
  150.2 3.6 %fusion.82 = f32[4,256,512]{2,1,0:T(8,128)} fusion(bf16[4,256,512]{2,1,0:T(8,128)(2,1)} %get-tuple-element.190, f32[512]{0:T(512)S(1)} %bitcast.186, f32[4,256]{1,0:T(4,128)S(1)} %add_rsqrt_fusion.6, bf16[4,3,512,512]{3,2,1,0:T(8,128)(2,1)} %all-gather.4.cloned.1.call-done), kind=kOutput, calls=%fused_computation.119 | convolution fusion | flops 538968064 | bytes 3676160 | tf_op jit(solution)/shard_map/dot_general | solution.py:19
  153.8 3.1 %fusion.84 = f32[4,256,512]{2,1,0:T(8,128)} fusion(bf16[4,256,512]{2,1,0:T(8,128)(2,1)S(1)} %copy-done.15, f32[512]{0:T(512)S(1)} %bitcast.187, f32[4,256]{1,0:T(4,128)S(1)} %add_rsqrt_fusion.6, bf16[4,3,512,512]{3,2,1,0:T(8,128)(2,1)} %all-gather.4.cloned.1.call-done), kind=kOutput, calls=%fused_computation.120 | convolution fusion | flops 538968064 | bytes 3676160 | tf_op jit(solution)/shard_map/dot_general | solution.py:19
  156.9 4.3 %fusion.19 = bf16[4,256,512]{2,1,0:T(8,128)(2,1)S(1)} fusion(bf16[4,256,512]{2,1,0:T(8,128)(2,1)} %get-tuple-element.190, f32[4,256,512]{2,1,0:T(8,128)} %fusion.82, f32[4,256,512]{2,1,0:T(8,128)} %fusion.84, f32[512]{0:T(512)S(1)} %bitcast.188, f32[4,256]{1,0:T(4,128)S(1)} %add_rsqrt_fusion.6, bf16[4,3,512,512]{3,2,1,0:T(8,128)(2,1)} %all-gather.4.cloned.1.call-done, ...), kind=kOutput, calls=%fused_computation.57 | convolution fusion | flops 1081081856 | bytes 8394752 | tf_op jit(solution)/shard_map/dot_general | solution.py:25
  161.3 1.1 fusion.125
  163.0 0.6 fusion.142
  163.6 0.7 broadcast_select_fusion.9
  164.3 0.1 fusion.143
  164.4 0.2 fusion.155
  164.6 39.3 %all-reduce.16 = (f32[8,18]{1,0:T(8,128)S(1)}, f32[8]{0:T(128)S(1)}) all-reduce(f32[8,18]{1,0:T(8,128)S(1)} %scatter-add.19, f32[8]{0:T(128)S(1)} %fusion.155), channel_id=1, replica_groups=mesh['section'=4,'dp'=8] {'section','dp'}, use_global_device_ids=true, to_apply=%region_18.20 | all-reduce | flops 152 | bytes 1216 | tf_op jit(solution)/shard_map/psum | solution.py:108
  203.9 0.7 broadcast_select_fusion.11
  204.7 0.6 broadcast_select_fusion.8
  205.3 0.7 broadcast_select_fusion.7
  206.1 0.6 broadcast_select_fusion.6
  206.7 0.6 broadcast_select_fusion.5
  207.4 0.7 broadcast_select_fusion.4
  208.1 0.7 broadcast_select_fusion.3
  208.9 0.6 broadcast_select_fusion.2
  209.5 0.1 fusion.139
  209.7 0.6 multiply_reduce_fusion.1
  210.3 0.6 multiply_reduce_fusion
  210.8 0.4 multiply_convert_fusion.7
  211.3 0.4 copy-done.2
  211.6 0.6 copy-done.4
  212.2 3.1 %fusion.120 = f32[4,256,512]{2,1,0:T(8,128)} fusion(bf16[4,256,512]{2,1,0:T(8,128)(2,1)S(1)} %bitcast.170, bf16[4,3,512,512]{3,2,1,0:T(8,128)(2,1)} %all-gather.4.cloned.1.call-done), kind=kOutput, calls=%fused_computation.160 | convolution fusion | flops 536870912 | bytes 3670016 | tf_op jit(solution)/shard_map/dot_general | solution.py:19
  215.3 3.1 %fusion.118 = f32[4,256,512]{2,1,0:T(8,128)} fusion(bf16[4,256,512]{2,1,0:T(8,128)(2,1)S(1)} %bitcast.171, bf16[4,3,512,512]{3,2,1,0:T(8,128)(2,1)} %all-gather.4.cloned.1.call-done), kind=kOutput, calls=%fused_computation.158 | convolution fusion | flops 536870912 | bytes 3670016 | tf_op jit(solution)/shard_map/dot_general | solution.py:19
  218.4 5.2 %fusion.28 = (f32[4,256]{1,0:T(4,128)S(1)}, bf16[4,256,512]{2,1,0:T(8,128)(2,1)}) fusion(f32[4,256,512]{2,1,0:T(8,128)} %bitcast.174, bf16[4,512,512]{2,1,0:T(8,128)(2,1)} %all-gather.6.cloned.1.call-done, f32[4,256,512]{2,1,0:T(8,128)} %fusion.120, f32[4,256,512]{2,1,0:T(8,128)} %fusion.118, bf16[4,256,512]{2,1,0:T(8,128)(2,1)S(1)} %bitcast.172, ...), kind=kOutput, calls=%fused_computation.66 | convolution fusion | flops 1080032256 | bytes 9441280 | tf_op jit(solution)/shard_map/dot_general | solution.py:25
  223.6 3.5 %fusion.48 = f32[4,256,512]{2,1,0:T(8,128)} fusion(bf16[4,256,512]{2,1,0:T(8,128)(2,1)} %get-tuple-element.196, f32[4,256]{1,0:T(4,128)S(1)} %add_rsqrt_fusion, f32[512]{0:T(512)S(1)} %bitcast.177, bf16[4,3,512,512]{3,2,1,0:T(8,128)(2,1)} %all-gather.4.cloned.1.call-done), kind=kOutput, calls=%fused_computation.103 | convolution fusion | flops 538968064 | bytes 3676160 | tf_op jit(solution)/shard_map/dot_general | solution.py:19
  227.1 3.2 %fusion.46 = f32[4,256,512]{2,1,0:T(8,128)} fusion(bf16[4,256,512]{2,1,0:T(8,128)(2,1)S(1)} %copy-done.14, f32[4,256]{1,0:T(4,128)S(1)} %add_rsqrt_fusion, f32[512]{0:T(512)S(1)} %bitcast.178, bf16[4,3,512,512]{3,2,1,0:T(8,128)(2,1)} %all-gather.4.cloned.1.call-done), kind=kOutput, calls=%fused_computation.102 | convolution fusion | flops 538968064 | bytes 3676160 | tf_op jit(solution)/shard_map/dot_general | solution.py:19
  230.3 3.8 %fusion.43 = f32[4,256]{1,0:T(4,128)S(1)} fusion(f32[4,256,512]{2,1,0:T(8,128)} %fusion.46, f32[4,256,512]{2,1,0:T(8,128)} %fusion.48, bf16[4,256,512]{2,1,0:T(8,128)(2,1)S(1)} %copy-done.14, f32[4,256]{1,0:T(4,128)S(1)} %add_rsqrt_fusion, f32[512]{0:T(512)S(1)} %bitcast.179, bf16[4,3,512,512]{3,2,1,0:T(8,128)(2,1)} %all-gather.4.cloned.1.call-done, ...), kind=kOutput, calls=%fused_computation.81 | convolution fusion | flops 1084226560 | bytes 8399360 | tf_op jit(solution)/shard_map/dot_general | solution.py:25
  234.0 3.0 %fusion.121 = f32[4,256,512]{2,1,0:T(8,128)} fusion(bf16[4,256,512]{2,1,0:T(8,128)(2,1)S(1)} %bitcast.167, bf16[4,3,512,512]{3,2,1,0:T(8,128)(2,1)} %all-gather.4.cloned.1.call-done), kind=kOutput, calls=%fused_computation.161 | convolution fusion | flops 536870912 | bytes 3670016 | tf_op jit(solution)/shard_map/dot_general | solution.py:19
  237.1 3.3 %fusion.119 = f32[4,256,512]{2,1,0:T(8,128)} fusion(bf16[4,256,512]{2,1,0:T(8,128)(2,1)S(1)} %bitcast.168, bf16[4,3,512,512]{3,2,1,0:T(8,128)(2,1)} %all-gather.4.cloned.1.call-done), kind=kOutput, calls=%fused_computation.159 | convolution fusion | flops 536870912 | bytes 3670016 | tf_op jit(solution)/shard_map/dot_general | solution.py:19
  240.3 4.4 %fusion.20 = (f32[4,256]{1,0:T(4,128)S(1)}, bf16[4,256,512]{2,1,0:T(8,128)(2,1)}) fusion(f32[4,256,512]{2,1,0:T(8,128)S(1)} %bitcast.173, bf16[4,512,512]{2,1,0:T(8,128)(2,1)} %all-gather.6.cloned.1.call-done, f32[4,256,512]{2,1,0:T(8,128)} %fusion.121, f32[4,256,512]{2,1,0:T(8,128)} %fusion.119, bf16[4,256,512]{2,1,0:T(8,128)(2,1)S(1)} %bitcast.169, ...), kind=kOutput, calls=%fused_computation.58 | convolution fusion | flops 1080032256 | bytes 9441280 | tf_op jit(solution)/shard_map/dot_general | solution.py:25
  244.7 3.6 %fusion.68 = f32[4,256,512]{2,1,0:T(8,128)} fusion(bf16[4,256,512]{2,1,0:T(8,128)(2,1)} %get-tuple-element.198, f32[512]{0:T(512)S(1)} %bitcast.180, f32[4,256]{1,0:T(4,128)S(1)} %add_rsqrt_fusion.4, bf16[4,3,512,512]{3,2,1,0:T(8,128)(2,1)} %all-gather.4.cloned.1.call-done), kind=kOutput, calls=%fused_computation.111 | convolution fusion | flops 538968064 | bytes 3676160 | tf_op jit(solution)/shard_map/dot_general | solution.py:19
  248.4 3.2 %fusion.70 = f32[4,256,512]{2,1,0:T(8,128)} fusion(bf16[4,256,512]{2,1,0:T(8,128)(2,1)S(1)} %copy-done.13, f32[512]{0:T(512)S(1)} %bitcast.181, f32[4,256]{1,0:T(4,128)S(1)} %add_rsqrt_fusion.4, bf16[4,3,512,512]{3,2,1,0:T(8,128)(2,1)} %all-gather.4.cloned.1.call-done), kind=kOutput, calls=%fused_computation.112 | convolution fusion | flops 538968064 | bytes 3676160 | tf_op jit(solution)/shard_map/dot_general | solution.py:19
  251.6 3.8 %fusion.37 = f32[4,256]{1,0:T(4,128)S(1)} fusion(f32[4,256,512]{2,1,0:T(8,128)} %fusion.68, f32[4,256,512]{2,1,0:T(8,128)} %fusion.70, bf16[4,256,512]{2,1,0:T(8,128)(2,1)S(1)} %copy-done.13, f32[512]{0:T(512)S(1)} %bitcast.182, f32[4,256]{1,0:T(4,128)S(1)} %add_rsqrt_fusion.4, bf16[4,3,512,512]{3,2,1,0:T(8,128)(2,1)} %all-gather.4.cloned.1.call-done, ...), kind=kOutput, calls=%fused_computation.75 | convolution fusion | flops 1084226560 | bytes 8399360 | tf_op jit(solution)/shard_map/dot_general | solution.py:25
  255.3 0.5 negate_subtract_fusion
  255.8 0.6 pad_maximum_fusion
  (59 shorter events, 0.5 us)
Async XLA Ops:
  7.2 202.5 %copy-start = (bf16[18,512]{1,0:T(8,128)(2,1)S(1)}, bf16[18,512]{1,0:T(8,128)(2,1)}, u32[]{:S(2)}) copy-start(bf16[18,512]{1,0:T(8,128)(2,1)} %param.43) | copy-start | bytes 55300
  7.2 1.5 copy-start.7
  7.2 12.6 %copy-start.8 = (s32[8,4]{0,1:T(4,128)S(1)}, s32[8,4]{0,1:T(4,128)}, u32[]{:S(2)}) copy-start(s32[8,4]{0,1:T(4,128)} %param.36) | copy-start | bytes 388
  7.2 75.5 %all-gather.4.cloned.1.call-start = ((), (), s32[]{:S(2)}) async-start(), calls=%async_computation | async-start | bytes 7864320 | tf_op jit(solution)/shard_map/all_gather | solution.py:89
  7.9 111.8 %all-gather.6.cloned.1.call-start = ((), (), s32[]{:S(2)}) async-start(), calls=%async_computation.1 | async-start | bytes 2621440 | tf_op jit(solution)/shard_map/all_gather | solution.py:90
  20.1 14.6 %copy-start.10 = (bf16[1,512]{1,0:T(2,128)(2,1)S(1)}, bf16[1,512]{1,0:T(2,128)(2,1)}, u32[]{:S(2)}) copy-start(bf16[1,512]{1,0:T(2,128)(2,1)} %param.40) | copy-start | bytes 3076
  20.1 23.9 %copy-start.9 = (s32[2]{0:T(128)S(1)}, s32[2]{0:T(128)}, u32[]{:S(2)}) copy-start(s32[2]{0:T(128)} %constant.321.clone.1) | copy-start | bytes 28
  25.0 120.6 %copy-start.5 = (bf16[4,256,512]{2,1,0:T(8,128)(2,1)}, bf16[4,256,512]{2,1,0:T(8,128)(2,1)S(1)}, u32[]{:S(2)}) copy-start(bf16[4,256,512]{2,1,0:T(8,128)(2,1)S(1)} %gather_fusion) | copy-start | bytes 3145732
  124.3 3.5 %copy-start.16 = (bf16[4,256,512]{2,1,0:T(8,128)(2,1)S(1)}, bf16[4,256,512]{2,1,0:T(8,128)(2,1)}, u32[]{:S(2)}) copy-start(bf16[4,256,512]{2,1,0:T(8,128)(2,1)} %get-tuple-element.188) | copy-start | bytes 3145732
  131.1 5.2 %copy-start.11 = (bf16[512,18]{0,1:T(8,128)(2,1)S(1)}, bf16[512,18]{0,1:T(8,128)(2,1)}, u32[]{:S(2)}) copy-start(bf16[512,18]{0,1:T(8,128)(2,1)} %param.41) | copy-start | bytes 55300
  131.1 5.2 %copy-start.12 = (f32[18]{0:T(128)S(1)}, f32[18]{0:T(128)}, u32[]{:S(2)}) copy-start(f32[18]{0:T(128)} %param.42) | copy-start | bytes 220
  150.2 3.6 %copy-start.15 = (bf16[4,256,512]{2,1,0:T(8,128)(2,1)S(1)}, bf16[4,256,512]{2,1,0:T(8,128)(2,1)}, u32[]{:S(2)}) copy-start(bf16[4,256,512]{2,1,0:T(8,128)(2,1)} %get-tuple-element.190) | copy-start | bytes 3145732
  210.2 1.4 copy-start.2
  210.8 1.4 copy-start.4
  223.6 3.5 %copy-start.14 = (bf16[4,256,512]{2,1,0:T(8,128)(2,1)S(1)}, bf16[4,256,512]{2,1,0:T(8,128)(2,1)}, u32[]{:S(2)}) copy-start(bf16[4,256,512]{2,1,0:T(8,128)(2,1)} %get-tuple-element.196) | copy-start | bytes 3145732
  237.1 3.3 %copy-start.3 = (f32[1024,512]{1,0:T(8,128)S(1)}, f32[1024,512]{1,0:T(8,128)}, u32[]{:S(2)}) copy-start(f32[1024,512]{1,0:T(8,128)} %copy-done.2) | copy-start | bytes 6291460
  244.7 3.6 %copy-start.13 = (bf16[4,256,512]{2,1,0:T(8,128)(2,1)S(1)}, bf16[4,256,512]{2,1,0:T(8,128)(2,1)}, u32[]{:S(2)}) copy-start(bf16[4,256,512]{2,1,0:T(8,128)(2,1)} %get-tuple-element.198) | copy-start | bytes 3145732
  248.4 3.2 %copy-start.6 = (bf16[4,256,512]{2,1,0:T(8,128)(2,1)S(1)}, bf16[4,256,512]{2,1,0:T(8,128)(2,1)}, u32[]{:S(2)}) copy-start(bf16[4,256,512]{2,1,0:T(8,128)(2,1)} %copy-done.5) | copy-start | bytes 3145732
  251.5 4.9 %copy-start.1 = (bf16[18,512]{1,0:T(8,128)(2,1)S(1)}, bf16[18,512]{1,0:T(8,128)(2,1)}, u32[]{:S(2)}) copy-start(bf16[18,512]{1,0:T(8,128)(2,1)} %param.43) | copy-start | bytes 55300
Sparse Core Ops, SparseCore 0:
  9.9 72.7 all-gather.3
  84.5 35.1 all-gather.5
where the time goes:
time: 265 us; the launch traced here: 263 us
  matrix products  92.5 us (35%)
  waiting for transfers between devices  68.2 us (26%)
  blocking collectives  48.6 us (18%)
  between operations  31.2 us (12%)
  local copies, waits for them, and re-layouts  11.6 us (4%)
  other arithmetic  11.1 us (4%)
    dot_general x16, matrix products, run_block(): jnp.dot(flat, tap_set[k], preferred_element_type=jnp.float32)  52 us
    psum x1, blocking collectives, on_device(): lax.psum((bit_buffer, entropy_buffer), ('section', 'dp'))  39.3 us
    all_gather x1, waiting for transfers between devices, on_device(): lax.all_gather(tap_weights, 'section', axis=0, tiled=True)  36.1 us
    dot_general x8, matrix products, run_block(): jnp.dot(activated.reshape(-1, channels), out_weight, preferred_element_ty...  35.9 us
    all_gather x1, waiting for transfers between devices, on_device(): lax.all_gather(out_weights, 'section', axis=0, tiled=True)  30.7 us
    all_gather x1, blocking collectives, on_device(): lax.all_gather(norm_gains, 'section', axis=0, tiled=True)  9.32 us
    gather x2, local copies, waits for them, and re-layouts, on_device(): source = jnp.take(clip_pool, clip_index[batch_slot], axis=0)  9.28 us
    another operation x12, other arithmetic  8.18 us
  transfers between devices with their start and end apart: 2, of which 2 were waited for; matrix products, arithmetic and copies ran while one was open for 7% of the time, Pallas kernels for 0%

commit v1 on v0

--- a/solution.py
+++ b/solution.py
@@ -85,9 +85,15 @@
     rows_total = float(clip_count * lax.axis_size("dp") * row_count)
     bit_buffer = jnp.zeros((batches, quant_weight.shape[1]), jnp.float32)
     entropy_buffer = jnp.zeros((batches,), jnp.float32)
+    update_tracks_on = lambda x_in, mesh_name: jnp.concatenate(
+        lax.all_to_all(
+            jnp.stack([x_in for _ in range(lax.psum(1, mesh_name))], axis=0), mesh_name, 0, 0
+        ),
+        0,
+    )
     all_taps, all_out, all_gains = (
         lax.all_gather(tap_weights, "section", axis=0, tiled=True),
-        lax.all_gather(out_weights, "section", axis=0, tiled=True),
+        update_tracks_on(out_weights, "section"),
         lax.all_gather(norm_gains, "section", axis=0, tiled=True),
     )
     per_section = batches // sections

time: 265 us -> 254 us (0.958)
  waiting for transfers between devices: 68.2 us -> 36.9 us
  blocking collectives: 48.6 us -> 60.8 us
  starting transfers between devices: 0.08 us -> 5.36 us
    all_gather x1 -> x0, waiting for transfers between devices: 30.7 us -> none  [on_device(): lax.all_gather(out_weights, 'section', axis=0, tiled=True)]
    all_gather x1, blocking collectives: 9.32 us -> 21.5 us  [on_device(): lax.all_gather(norm_gains, 'section', axis=0, tiled=True)]
    all_to_all x0 -> x1, starting transfers between devices: none -> 5.32 us  [on_device(): lax.all_to_all(jnp.stack([x_in for _ in range(lax.psum(1, mesh_name))], a...]
  transfers between devices with their start and end apart: 2 -> 2, of which waited for: 2 -> 1; matrix products, arithmetic and copies ran while one was open for 7% -> 8% of each run, Pallas kernels for 0% -> 0%
where the time goes in v1:
time: 254 us; the launch traced here: 252 us
  matrix products  94.9 us (37%)
  blocking collectives  60.8 us (24%)
  waiting for transfers between devices  36.9 us (15%)
  between operations  30.4 us (12%)
  local copies, waits for them, and re-layouts  13.2 us (5%)
  other arithmetic  10.9 us (4%)
  starting transfers between devices  5.36 us (2%)
    dot_general x16, matrix products, run_block(): jnp.dot(flat, tap_set[k], preferred_element_type=jnp.float32)  52.2 us
    psum x1, blocking collectives, on_device(): lax.psum((bit_buffer, entropy_buffer), ('section', 'dp'))  39.3 us
    dot_general x8, matrix products, run_block(): jnp.dot(activated.reshape(-1, channels), out_weight, preferred_element_ty...  36.8 us
    all_gather x1, waiting for transfers between devices, on_device(): lax.all_gather(tap_weights, 'section', axis=0, tiled=True)  36.3 us
    all_gather x1, blocking collectives, on_device(): lax.all_gather(norm_gains, 'section', axis=0, tiled=True)  21.5 us
    gather x2, local copies, waits for them, and re-layouts, on_device(): source = jnp.take(clip_pool, clip_index[batch_slot], axis=0)  8.37 us
    another operation x12, other arithmetic  8.04 us
    all_to_all x1, starting transfers between devices, on_device(): lax.all_to_all(jnp.stack([x_in for _ in range(lax.psum(1, mesh_name))], a...  5.32 us
  transfers between devices with their start and end apart: 2, of which 1 were waited for; matrix products, arithmetic and copies ran while one was open for 8% of the time, Pallas kernels for 0%

profile of v1, /device:TPU:0, one launch (start us, length us, event | category | flops | bytes accessed | tf_op | source)
XLA Modules:
  0.0 252.5 jit_solution(12421077134038402218)
XLA Ops:
  7.2 0.0 copy-start
  7.2 0.0 all-gather.3.cloned.1.call-start
  7.2 0.7 all-gather.3.cloned.1.call-update
  7.9 2.6 %stack.4 = bf16[4,1,512,512]{3,2,1,0:T(8,128)(2,1)} broadcast(bf16[512,512]{1,0:T(8,128)(2,1)} %bitcast.180), dimensions={2,3} | broadcast | bytes 2621440 | tf_op jit(solution)/shard_map/stack | solution.py:90
  10.5 5.3 %all-to-all-start = ((bf16[4,1,512,512]{3,2,1,0:T(8,128)(2,1)}), bf16[4,1,512,512]{3,2,1,0:T(8,128)(2,1)}, u32[]{:S(2)}, u32[]{:S(2)}) async-start(bf16[4,1,512,512]{3,2,1,0:T(8,128)(2,1)} %stack.4), calls=%async_computation | async-start | bytes 4194304 | tf_op jit(solution)/shard_map/all_to_all | solution.py:89
  15.8 0.7 fusion.181
  26.4 0.2 fusion.140
  26.7 0.0 copy-start.10
  26.7 0.0 copy-start.9
  26.7 4.0 %gather_fusion = bf16[4,256,512]{2,1,0:T(8,128)(2,1)S(1)} fusion(bf16[32,256,512]{2,1,0:T(8,128)(2,1)} %param.35, s32[1024]{0:T(1024)S(1)} %pad_clamp_fusion.1), kind=kCustom, calls=%fused_computation.clone | custom fusion | bytes 2097168 | tf_op jit(solution)/shard_map/jit(_take)/gather | solution.py:103
  30.7 4.4 %gather_fusion.1 = bf16[4,256,512]{2,1,0:T(8,128)(2,1)S(1)} fusion(bf16[32,256,512]{2,1,0:T(8,128)(2,1)} %param.35, s32[1024]{0:T(1024)S(1)} %pad_clamp_fusion), kind=kCustom, calls=%fused_computation.1.clone | custom fusion | bytes 2097168 | tf_op jit(solution)/shard_map/jit(_take)/gather | solution.py:103
  40.1 21.5 %all-gather = bf16[4,1,512]{2,1,0:T(2,128)(2,1)S(1)} all-gather(bf16[1,1,512]{2,1,0:T(2,128)(2,1)S(1)} %bitcast.182), channel_id=1, replica_groups=mesh['section'=4,'dp'=8] {'section'}, dimensions={0}, use_global_device_ids=true | all-gather | bytes 5120 | tf_op jit(solution)/shard_map/all_gather | solution.py:97
  61.6 0.9 and_reduce_fusion
  62.4 0.4 fusion.32
  62.9 0.8 and_reduce_fusion.4
  63.7 0.4 fusion.38
  64.1 36.3 %all-gather.3.cloned.1.call-done = bf16[4,3,512,512]{3,2,1,0:T(8,128)(2,1)} async-done(((bf16[1,3,512,512]{3,2,1,0:T(8,128)(2,1)}), bf16[4,3,512,512]{3,2,1,0:T(8,128)(2,1)}) %all-gather.3.cloned.1.call-update) | async-done | bytes 6291472 | tf_op jit(solution)/shard_map/all_gather | solution.py:95
  100.4 3.1 %fusion.104 = f32[4,256,512]{2,1,0:T(8,128)} fusion(f32[512]{0:T(512)S(1)} %bitcast.195, f32[4,256]{1,0:T(4,128)S(1)} %add_rsqrt_fusion.7, bf16[4,3,512,512]{3,2,1,0:T(8,128)(2,1)} %all-gather.3.cloned.1.call-done, bf16[4,256,512]{2,1,0:T(8,128)(2,1)S(1)} %gather_fusion, pred[4]{0:T(512)(128)(4,1)S(1)} %get-tuple-element.204), kind=kOutput, calls=%fused_computation.135 | convolution fusion | flops 539492352 | bytes 3676164 | tf_op jit(solution)/shard_map/dot_general | solution.py:19
  103.5 3.2 %fusion.106 = f32[4,256,512]{2,1,0:T(8,128)} fusion(f32[512]{0:T(512)S(1)} %bitcast.196, f32[4,256]{1,0:T(4,128)S(1)} %add_rsqrt_fusion.7, bf16[4,3,512,512]{3,2,1,0:T(8,128)(2,1)} %all-gather.3.cloned.1.call-done, bf16[4,256,512]{2,1,0:T(8,128)(2,1)S(1)} %gather_fusion, pred[4]{0:T(512)(128)(4,1)S(1)} %get-tuple-element.204), kind=kOutput, calls=%fused_computation.136 | convolution fusion | flops 539492352 | bytes 3676164 | tf_op jit(solution)/shard_map/dot_general | solution.py:19
  106.7 4.5 %fusion.16 = (f32[4,256]{1,0:T(4,128)S(1)}, bf16[4,256,512]{2,1,0:T(8,128)(2,1)}) fusion(bf16[4,1,512,512]{3,2,1,0:T(8,128)(2,1)} %all-to-all-done, f32[4,256,512]{2,1,0:T(8,128)} %fusion.104, f32[4,256,512]{2,1,0:T(8,128)} %fusion.106, f32[512]{0:T(512)S(1)} %bitcast.197, f32[4,256]{1,0:T(4,128)S(1)} %add_rsqrt_fusion.7, ...), kind=kOutput, calls=%fused_computation.54 | convolution fusion | flops 1083702272 | bytes 8399872 | tf_op jit(solution)/shard_map/dot_general | solution.py:25
  111.2 3.1 %fusion.60 = f32[4,256,512]{2,1,0:T(8,128)} fusion(f32[4,256]{1,0:T(4,128)S(1)} %add_rsqrt_fusion.3, f32[512]{0:T(512)S(1)} %bitcast.198, bf16[4,3,512,512]{3,2,1,0:T(8,128)(2,1)} %all-gather.3.cloned.1.call-done, bf16[4,256,512]{2,1,0:T(8,128)(2,1)S(1)} %gather_fusion.1, pred[4]{0:T(512)(128)(4,1)S(1)} %get-tuple-element.203), kind=kOutput, calls=%fused_computation.107 | convolution fusion | flops 539492352 | bytes 3676164 | tf_op jit(solution)/shard_map/dot_general | solution.py:19
  114.3 3.2 %fusion.58 = f32[4,256,512]{2,1,0:T(8,128)} fusion(f32[4,256]{1,0:T(4,128)S(1)} %add_rsqrt_fusion.3, f32[512]{0:T(512)S(1)} %bitcast.199, bf16[4,3,512,512]{3,2,1,0:T(8,128)(2,1)} %all-gather.3.cloned.1.call-done, bf16[4,256,512]{2,1,0:T(8,128)(2,1)S(1)} %gather_fusion.1, pred[4]{0:T(512)(128)(4,1)S(1)} %get-tuple-element.203), kind=kOutput, calls=%fused_computation.106 | convolution fusion | flops 539492352 | bytes 3676164 | tf_op jit(solution)/shard_map/dot_general | solution.py:19
  117.5 4.6 %fusion.24 = (f32[4,256]{1,0:T(4,128)S(1)}, bf16[4,256,512]{2,1,0:T(8,128)(2,1)}) fusion(bf16[4,1,512,512]{3,2,1,0:T(8,128)(2,1)} %all-to-all-done, f32[4,256,512]{2,1,0:T(8,128)} %fusion.58, f32[4,256,512]{2,1,0:T(8,128)} %fusion.60, f32[4,256]{1,0:T(4,128)S(1)} %add_rsqrt_fusion.3, f32[512]{0:T(512)S(1)} %bitcast.200, ...), kind=kOutput, calls=%fused_computation.62 | convolution fusion | flops 1083702272 | bytes 8399872 | tf_op jit(solution)/shard_map/dot_general | solution.py:25
  122.1 3.5 %fusion.54 = f32[4,256,512]{2,1,0:T(8,128)} fusion(bf16[4,256,512]{2,1,0:T(8,128)(2,1)} %get-tuple-element.188, f32[4,256]{1,0:T(4,128)S(1)} %add_rsqrt_fusion.2, f32[512]{0:T(512)S(1)} %bitcast.189, bf16[4,3,512,512]{3,2,1,0:T(8,128)(2,1)} %all-gather.3.cloned.1.call-done), kind=kOutput, calls=%fused_computation.105 | convolution fusion | flops 538968064 | bytes 3676160 | tf_op jit(solution)/shard_map/dot_general | solution.py:19
  125.6 3.2 %fusion.52 = f32[4,256,512]{2,1,0:T(8,128)} fusion(bf16[4,256,512]{2,1,0:T(8,128)(2,1)S(1)} %copy-done.15, f32[4,256]{1,0:T(4,128)S(1)} %add_rsqrt_fusion.2, f32[512]{0:T(512)S(1)} %bitcast.190, bf16[4,3,512,512]{3,2,1,0:T(8,128)(2,1)} %all-gather.3.cloned.1.call-done), kind=kOutput, calls=%fused_computation.104 | convolution fusion | flops 538968064 | bytes 3676160 | tf_op jit(solution)/shard_map/dot_general | solution.py:19
  128.8 5.2 %fusion.27 = bf16[4,256,512]{2,1,0:T(8,128)(2,1)} fusion(bf16[4,256,512]{2,1,0:T(8,128)(2,1)} %get-tuple-element.188, f32[4,256,512]{2,1,0:T(8,128)} %fusion.52, f32[4,256,512]{2,1,0:T(8,128)} %fusion.54, f32[4,256]{1,0:T(4,128)S(1)} %add_rsqrt_fusion.2, f32[512]{0:T(512)S(1)} %bitcast.191, bf16[4,3,512,512]{3,2,1,0:T(8,128)(2,1)} %all-gather.3.cloned.1.call-done, ...), kind=kOutput, calls=%fused_computation.65 | convolution fusion | flops 1081081856 | bytes 8394752 | tf_op jit(solution)/shard_map/dot_general | solution.py:25
  134.1 2.3 fusion.131
  137.0 3.5 %fusion.82 = f32[4,256,512]{2,1,0:T(8,128)} fusion(bf16[4,256,512]{2,1,0:T(8,128)(2,1)} %get-tuple-element.190, f32[512]{0:T(512)S(1)} %bitcast.192, f32[4,256]{1,0:T(4,128)S(1)} %add_rsqrt_fusion.6, bf16[4,3,512,512]{3,2,1,0:T(8,128)(2,1)} %all-gather.3.cloned.1.call-done), kind=kOutput, calls=%fused_computation.119 | convolution fusion | flops 538968064 | bytes 3676160 | tf_op jit(solution)/shard_map/dot_general | solution.py:19
  140.5 3.4 %fusion.84 = f32[4,256,512]{2,1,0:T(8,128)} fusion(bf16[4,256,512]{2,1,0:T(8,128)(2,1)} %get-tuple-element.190, f32[512]{0:T(512)S(1)} %bitcast.193, f32[4,256]{1,0:T(4,128)S(1)} %add_rsqrt_fusion.6, bf16[4,3,512,512]{3,2,1,0:T(8,128)(2,1)} %all-gather.3.cloned.1.call-done), kind=kOutput, calls=%fused_computation.120 | convolution fusion | flops 538968064 | bytes 3676160 | tf_op jit(solution)/shard_map/dot_general | solution.py:19
  143.9 5.3 %fusion.19 = bf16[4,256,512]{2,1,0:T(8,128)(2,1)} fusion(bf16[4,256,512]{2,1,0:T(8,128)(2,1)} %get-tuple-element.190, f32[4,256,512]{2,1,0:T(8,128)} %fusion.82, f32[4,256,512]{2,1,0:T(8,128)} %fusion.84, f32[512]{0:T(512)S(1)} %bitcast.194, f32[4,256]{1,0:T(4,128)S(1)} %add_rsqrt_fusion.6, bf16[4,3,512,512]{3,2,1,0:T(8,128)(2,1)} %all-gather.3.cloned.1.call-done, ...), kind=kOutput, calls=%fused_computation.57 | convolution fusion | flops 1081081856 | bytes 8394752 | tf_op jit(solution)/shard_map/dot_general | solution.py:25
  149.3 2.4 fusion.125
  152.3 0.7 fusion.142
  153.1 0.6 broadcast_select_fusion.9
  153.7 0.1 fusion.143
  153.8 0.2 fusion.155
  154.0 39.3 %all-reduce.16 = (f32[8,18]{1,0:T(8,128)S(1)}, f32[8]{0:T(128)S(1)}) all-reduce(f32[8,18]{1,0:T(8,128)S(1)} %scatter-add.19, f32[8]{0:T(128)S(1)} %fusion.155), channel_id=1, replica_groups=mesh['section'=4,'dp'=8] {'section','dp'}, use_global_device_ids=true, to_apply=%region_18.20 | all-reduce | flops 152 | bytes 1216 | tf_op jit(solution)/shard_map/psum | solution.py:114
  193.3 0.7 broadcast_select_fusion.11
  194.1 0.6 broadcast_select_fusion.8
  194.7 0.6 broadcast_select_fusion.7
  195.4 0.6 broadcast_select_fusion.6
  196.0 0.6 broadcast_select_fusion.5
  196.7 0.6 broadcast_select_fusion.4
  197.4 0.6 broadcast_select_fusion.3
  198.1 0.6 broadcast_select_fusion.2
  198.7 0.1 fusion.139
  198.9 0.6 multiply_reduce_fusion.1
  199.5 0.6 multiply_reduce_fusion
  200.0 0.4 multiply_convert_fusion.7
  200.5 0.4 copy-done.2
  200.8 0.6 copy-done.4
  201.4 3.1 %fusion.120 = f32[4,256,512]{2,1,0:T(8,128)} fusion(bf16[4,256,512]{2,1,0:T(8,128)(2,1)S(1)} %bitcast.175, bf16[4,3,512,512]{3,2,1,0:T(8,128)(2,1)} %all-gather.3.cloned.1.call-done), kind=kOutput, calls=%fused_computation.160 | convolution fusion | flops 536870912 | bytes 3670016 | tf_op jit(solution)/shard_map/dot_general | solution.py:19
  204.5 3.1 %fusion.118 = f32[4,256,512]{2,1,0:T(8,128)} fusion(bf16[4,256,512]{2,1,0:T(8,128)(2,1)S(1)} %bitcast.176, bf16[4,3,512,512]{3,2,1,0:T(8,128)(2,1)} %all-gather.3.cloned.1.call-done), kind=kOutput, calls=%fused_computation.158 | convolution fusion | flops 536870912 | bytes 3670016 | tf_op jit(solution)/shard_map/dot_general | solution.py:19
  207.6 5.2 %fusion.28 = (f32[4,256]{1,0:T(4,128)S(1)}, bf16[4,256,512]{2,1,0:T(8,128)(2,1)}) fusion(f32[4,256,512]{2,1,0:T(8,128)} %bitcast.179, bf16[4,1,512,512]{3,2,1,0:T(8,128)(2,1)} %all-to-all-done, f32[4,256,512]{2,1,0:T(8,128)} %fusion.120, f32[4,256,512]{2,1,0:T(8,128)} %fusion.118, bf16[4,256,512]{2,1,0:T(8,128)(2,1)S(1)} %bitcast.177, ...), kind=kOutput, calls=%fused_computation.66 | convolution fusion | flops 1080032256 | bytes 9441280 | tf_op jit(solution)/shard_map/dot_general | solution.py:25
  212.8 3.5 %fusion.48 = f32[4,256,512]{2,1,0:T(8,128)} fusion(bf16[4,256,512]{2,1,0:T(8,128)(2,1)} %get-tuple-element.196, f32[4,256]{1,0:T(4,128)S(1)} %add_rsqrt_fusion, f32[512]{0:T(512)S(1)} %bitcast.183, bf16[4,3,512,512]{3,2,1,0:T(8,128)(2,1)} %all-gather.3.cloned.1.call-done), kind=kOutput, calls=%fused_computation.103 | convolution fusion | flops 538968064 | bytes 3676160 | tf_op jit(solution)/shard_map/dot_general | solution.py:19
  216.3 3.2 %fusion.46 = f32[4,256,512]{2,1,0:T(8,128)} fusion(bf16[4,256,512]{2,1,0:T(8,128)(2,1)S(1)} %copy-done.14, f32[4,256]{1,0:T(4,128)S(1)} %add_rsqrt_fusion, f32[512]{0:T(512)S(1)} %bitcast.184, bf16[4,3,512,512]{3,2,1,0:T(8,128)(2,1)} %all-gather.3.cloned.1.call-done), kind=kOutput, calls=%fused_computation.102 | convolution fusion | flops 538968064 | bytes 3676160 | tf_op jit(solution)/shard_map/dot_general | solution.py:19
  219.5 3.8 %fusion.43 = f32[4,256]{1,0:T(4,128)S(1)} fusion(f32[4,256,512]{2,1,0:T(8,128)} %fusion.46, f32[4,256,512]{2,1,0:T(8,128)} %fusion.48, bf16[4,256,512]{2,1,0:T(8,128)(2,1)S(1)} %copy-done.14, f32[4,256]{1,0:T(4,128)S(1)} %add_rsqrt_fusion, f32[512]{0:T(512)S(1)} %bitcast.185, bf16[4,3,512,512]{3,2,1,0:T(8,128)(2,1)} %all-gather.3.cloned.1.call-done, ...), kind=kOutput, calls=%fused_computation.81 | convolution fusion | flops 1084226560 | bytes 8399360 | tf_op jit(solution)/shard_map/dot_general | solution.py:25
  223.2 3.0 %fusion.121 = f32[4,256,512]{2,1,0:T(8,128)} fusion(bf16[4,256,512]{2,1,0:T(8,128)(2,1)S(1)} %bitcast.172, bf16[4,3,512,512]{3,2,1,0:T(8,128)(2,1)} %all-gather.3.cloned.1.call-done), kind=kOutput, calls=%fused_computation.161 | convolution fusion | flops 536870912 | bytes 3670016 | tf_op jit(solution)/shard_map/dot_general | solution.py:19
  226.3 3.3 %fusion.119 = f32[4,256,512]{2,1,0:T(8,128)} fusion(bf16[4,256,512]{2,1,0:T(8,128)(2,1)S(1)} %bitcast.173, bf16[4,3,512,512]{3,2,1,0:T(8,128)(2,1)} %all-gather.3.cloned.1.call-done), kind=kOutput, calls=%fused_computation.159 | convolution fusion | flops 536870912 | bytes 3670016 | tf_op jit(solution)/shard_map/dot_general | solution.py:19
  229.5 4.4 %fusion.20 = (f32[4,256]{1,0:T(4,128)S(1)}, bf16[4,256,512]{2,1,0:T(8,128)(2,1)}) fusion(f32[4,256,512]{2,1,0:T(8,128)S(1)} %bitcast.178, bf16[4,1,512,512]{3,2,1,0:T(8,128)(2,1)} %all-to-all-done, f32[4,256,512]{2,1,0:T(8,128)} %fusion.121, f32[4,256,512]{2,1,0:T(8,128)} %fusion.119, bf16[4,256,512]{2,1,0:T(8,128)(2,1)S(1)} %bitcast.174, ...), kind=kOutput, calls=%fused_computation.58 | convolution fusion | flops 1080032256 | bytes 9441280 | tf_op jit(solution)/shard_map/dot_general | solution.py:25
  234.0 3.6 %fusion.68 = f32[4,256,512]{2,1,0:T(8,128)} fusion(bf16[4,256,512]{2,1,0:T(8,128)(2,1)} %get-tuple-element.198, f32[512]{0:T(512)S(1)} %bitcast.186, f32[4,256]{1,0:T(4,128)S(1)} %add_rsqrt_fusion.4, bf16[4,3,512,512]{3,2,1,0:T(8,128)(2,1)} %all-gather.3.cloned.1.call-done), kind=kOutput, calls=%fused_computation.111 | convolution fusion | flops 538968064 | bytes 3676160 | tf_op jit(solution)/shard_map/dot_general | solution.py:19
  237.6 3.2 %fusion.70 = f32[4,256,512]{2,1,0:T(8,128)} fusion(bf16[4,256,512]{2,1,0:T(8,128)(2,1)S(1)} %copy-done.13, f32[512]{0:T(512)S(1)} %bitcast.187, f32[4,256]{1,0:T(4,128)S(1)} %add_rsqrt_fusion.4, bf16[4,3,512,512]{3,2,1,0:T(8,128)(2,1)} %all-gather.3.cloned.1.call-done), kind=kOutput, calls=%fused_computation.112 | convolution fusion | flops 538968064 | bytes 3676160 | tf_op jit(solution)/shard_map/dot_general | solution.py:19
  240.8 3.8 %fusion.37 = f32[4,256]{1,0:T(4,128)S(1)} fusion(f32[4,256,512]{2,1,0:T(8,128)} %fusion.68, f32[4,256,512]{2,1,0:T(8,128)} %fusion.70, bf16[4,256,512]{2,1,0:T(8,128)(2,1)S(1)} %copy-done.13, f32[512]{0:T(512)S(1)} %bitcast.188, f32[4,256]{1,0:T(4,128)S(1)} %add_rsqrt_fusion.4, bf16[4,3,512,512]{3,2,1,0:T(8,128)(2,1)} %all-gather.3.cloned.1.call-done, ...), kind=kOutput, calls=%fused_computation.75 | convolution fusion | flops 1084226560 | bytes 8399360 | tf_op jit(solution)/shard_map/dot_general | solution.py:25
  244.5 0.5 negate_subtract_fusion
  245.0 0.6 pad_maximum_fusion
  (57 shorter events, 0.5 us)
Async XLA Ops:
  7.2 191.7 %copy-start = (bf16[18,512]{1,0:T(8,128)(2,1)S(1)}, bf16[18,512]{1,0:T(8,128)(2,1)}, u32[]{:S(2)}) copy-start(bf16[18,512]{1,0:T(8,128)(2,1)} %param.43) | copy-start | bytes 55300
  7.2 93.2 %all-gather.3.cloned.1.call-start = ((), (), s32[]{:S(2)}) async-start(), calls=%async_computation.1 | async-start | bytes 7864320 | tf_op jit(solution)/shard_map/all_gather | solution.py:95
  10.5 5.3 %copy-start.7 = (s32[8]{0:T(128)S(1)}, s32[8]{0:T(128)}, u32[]{:S(2)}) copy-start(s32[8]{0:T(128)} %param.37) | copy-start | bytes 100
  10.5 15.9 %copy-start.8 = (s32[8,4]{0,1:T(4,128)S(1)}, s32[8,4]{0,1:T(4,128)}, u32[]{:S(2)}) copy-start(s32[8,4]{0,1:T(4,128)} %param.36) | copy-start | bytes 388
  10.5 96.1 %all-to-all-start = ((bf16[4,1,512,512]{3,2,1,0:T(8,128)(2,1)}), bf16[4,1,512,512]{3,2,1,0:T(8,128)(2,1)}, u32[]{:S(2)}, u32[]{:S(2)}) async-start(bf16[4,1,512,512]{3,2,1,0:T(8,128)(2,1)} %stack.4), calls=%async_computation | async-start | bytes 4194304 | tf_op jit(solution)/shard_map/all_to_all | solution.py:89
  26.7 13.4 %copy-start.10 = (bf16[1,512]{1,0:T(2,128)(2,1)S(1)}, bf16[1,512]{1,0:T(2,128)(2,1)}, u32[]{:S(2)}) copy-start(bf16[1,512]{1,0:T(2,128)(2,1)} %param.40) | copy-start | bytes 3076
  26.7 34.9 %copy-start.9 = (s32[2]{0:T(128)S(1)}, s32[2]{0:T(128)}, u32[]{:S(2)}) copy-start(s32[2]{0:T(128)} %constant.321.clone.1) | copy-start | bytes 28
  30.7 76.0 %copy-start.5 = (bf16[4,256,512]{2,1,0:T(8,128)(2,1)}, bf16[4,256,512]{2,1,0:T(8,128)(2,1)S(1)}, u32[]{:S(2)}) copy-start(bf16[4,256,512]{2,1,0:T(8,128)(2,1)S(1)} %gather_fusion) | copy-start | bytes 3145732
  122.1 3.5 %copy-start.15 = (bf16[4,256,512]{2,1,0:T(8,128)(2,1)S(1)}, bf16[4,256,512]{2,1,0:T(8,128)(2,1)}, u32[]{:S(2)}) copy-start(bf16[4,256,512]{2,1,0:T(8,128)(2,1)} %get-tuple-element.188) | copy-start | bytes 3145732
  128.8 5.2 %copy-start.11 = (bf16[512,18]{0,1:T(8,128)(2,1)S(1)}, bf16[512,18]{0,1:T(8,128)(2,1)}, u32[]{:S(2)}) copy-start(bf16[512,18]{0,1:T(8,128)(2,1)} %param.41) | copy-start | bytes 55300
  128.8 5.2 %copy-start.12 = (f32[18]{0:T(128)S(1)}, f32[18]{0:T(128)}, u32[]{:S(2)}) copy-start(f32[18]{0:T(128)} %param.42) | copy-start | bytes 220
  199.4 1.4 copy-start.2
  200.0 1.4 copy-start.4
  212.8 3.5 %copy-start.14 = (bf16[4,256,512]{2,1,0:T(8,128)(2,1)S(1)}, bf16[4,256,512]{2,1,0:T(8,128)(2,1)}, u32[]{:S(2)}) copy-start(bf16[4,256,512]{2,1,0:T(8,128)(2,1)} %get-tuple-element.196) | copy-start | bytes 3145732
  226.3 3.3 %copy-start.3 = (f32[1024,512]{1,0:T(8,128)S(1)}, f32[1024,512]{1,0:T(8,128)}, u32[]{:S(2)}) copy-start(f32[1024,512]{1,0:T(8,128)} %copy-done.2) | copy-start | bytes 6291460
  233.9 3.6 %copy-start.13 = (bf16[4,256,512]{2,1,0:T(8,128)(2,1)S(1)}, bf16[4,256,512]{2,1,0:T(8,128)(2,1)}, u32[]{:S(2)}) copy-start(bf16[4,256,512]{2,1,0:T(8,128)(2,1)} %get-tuple-element.198) | copy-start | bytes 3145732
  237.6 3.2 %copy-start.6 = (bf16[4,256,512]{2,1,0:T(8,128)(2,1)S(1)}, bf16[4,256,512]{2,1,0:T(8,128)(2,1)}, u32[]{:S(2)}) copy-start(bf16[4,256,512]{2,1,0:T(8,128)(2,1)} %copy-done.5) | copy-start | bytes 3145732
  240.8 4.9 %copy-start.1 = (bf16[18,512]{1,0:T(8,128)(2,1)S(1)}, bf16[18,512]{1,0:T(8,128)(2,1)}, u32[]{:S(2)}) copy-start(bf16[18,512]{1,0:T(8,128)(2,1)} %param.43) | copy-start | bytes 55300
Sparse Core Ops, SparseCore 0:
  9.8 90.4 all-gather.2
